TPU v7x, 32 devices: a whole 2x2x4 slice. The times are simulated.
32 devices in a mesh: feat: 8 (over y, x, core), rep: 4 (over z).
Axes of the slice: x: 2, y: 2, z: 4, core: 2. Of those that a mesh axis runs over, the one named last changes fastest.
Arguments:
- features: bfloat16 [4, 8, 1024, 512], P('rep', None, 'feat'), may hold values from -6 to 6
- adjacency_one: int32 [4, 8, 5, 16, 512], P('rep'), may hold values from 0 to 65535, as said below
- pre_hidden: bfloat16 [4, 8, 256, 256], P('rep', 'feat'), may hold values from -6 to 6
- adjacency_two: int32 [4, 8, 5, 8, 256], P('rep', 'feat'), may hold values from 0 to 65535, as said below
- weight_two: bfloat16 [6, 256, 256], replicated, may hold values from -0.375 to 0.375
- out_grad: bfloat16 [4, 8, 128, 256], P('rep', 'feat'), may hold values from -6 to 6
Outputs:
- grad_w1: float32 [6, 1024, 256], P(None, 'feat')
- grad_b1: float32 [256], replicated
- grad_w2: float32 [6, 256, 256], replicated
- grad_b2: float32 [256], replicated
Inputs may be any that keep to these rules, and one draw needn't show every extreme that they name: `adjacency_one`: bit k, k below 16, of word (w, n) is the entry of destination row 16 w + k and source column n; higher bits are zero; some rows are empty. `adjacency_two`: bit k, k below 16, of word (w, n) is the entry of seed row 16 w + k and source column n; higher bits are zero; some rows are empty.
All inputs are finite; a program needn't handle non-finite values.
Results may differ from a plain program's by a relative error of at most 0.0041.
Values may be sent and summed in bfloat16 or wider, within the bound.
No kernel may reach another device: no remote copies, remote signals or barrier semaphores. Data moves between devices by JAX's collectives and lax.ppermute only.
A program may use at most 128 MiB of HBM per device.

v0:
```python
import math
import jax
import jax.numpy as jnp
from jax import lax
from jax.sharding import PartitionSpec as P


def unpack(packed):
    shifts = jnp.arange(16, dtype=jnp.int32)
    spread = jnp.bitwise_and(jnp.right_shift(packed[..., None, :], shifts[:, None]), 1)
    dense = spread.reshape(packed.shape[:-2] + (packed.shape[-2] * 16, packed.shape[-1]))
    degree = jnp.sum(dense, axis=-1).astype(jnp.float32)
    return (dense.astype(jnp.bfloat16), 1.0 / jnp.maximum(degree, 1.0))


def upper_layer(pre_rows, words_two, grad_rows, weight_two, factor):
    hidden = jnp.maximum(pre_rows, 0)
    seed_count = grad_rows.shape[0]
    matrix, inverse = unpack(words_two)
    mixed = (
        jnp.einsum("rsd,dh->rsh", matrix, hidden, preferred_element_type=jnp.float32)
        * inverse[..., None]
    ).astype(jnp.bfloat16)
    scaled = grad_rows.astype(jnp.float32) * factor
    scaled_low = scaled.astype(jnp.bfloat16)
    grad_rel = jnp.einsum("rsh,sk->rhk", mixed, scaled_low, preferred_element_type=jnp.float32)
    grad_self = jnp.einsum(
        "sh,sk->hk", hidden[:seed_count], scaled_low, preferred_element_type=jnp.float32
    )
    weight_grad = jnp.concatenate([grad_self[None], grad_rel], 0)
    backed = (
        jnp.einsum("sk,rhk->rsh", scaled_low, weight_two[1:], preferred_element_type=jnp.float32)
        * inverse[..., None]
    ).astype(jnp.bfloat16)
    spread_back = jnp.einsum("rsd,rsh->dh", matrix, backed, preferred_element_type=jnp.float32)
    own_part = jnp.einsum(
        "sk,hk->sh", scaled_low, weight_two[0], preferred_element_type=jnp.float32
    )
    hidden_total = spread_back + jnp.pad(own_part, ((0, hidden.shape[0] - seed_count), (0, 0)))
    hidden_grad = jnp.where(pre_rows > 0, hidden_total, 0.0).astype(jnp.bfloat16)
    return (
        weight_grad,
        jnp.sum(scaled, 0),
        hidden_grad,
        jnp.sum(hidden_grad.astype(jnp.float32), 0),
    )


def panel_terms(word_block, column_block, grad_block):
    matrix, inverse = unpack(word_block)
    rows_one = grad_block.shape[1]
    gathered = (
        jnp.einsum("brdn,bcn->brdc", matrix, column_block, preferred_element_type=jnp.float32)
        * inverse[..., None]
    ).astype(jnp.bfloat16)
    panel_rel = jnp.einsum(
        "brdc,bdh->rch", gathered, grad_block, preferred_element_type=jnp.float32
    )
    panel_self = jnp.einsum(
        "bcd,bdh->ch", column_block[:, :, :rows_one], grad_block, preferred_element_type=jnp.float32
    )
    return jnp.concatenate([panel_self[None], panel_rel], 0)


def on_device(features, adjacency_one, pre_hidden, adjacency_two, weight_two, out_grad):
    seed_count = out_grad.shape[2]
    factor = float(seed_count * lax.axis_size("feat") * lax.axis_size("rep")) ** (-0.5)
    weight_grad, bias_two, hidden_grad, bias_one = upper_layer(
        pre_hidden[0, 0], adjacency_two[0, 0], out_grad[0, 0], weight_two, factor
    )
    feature_local = features[0]
    adj_local = adjacency_one[0]
    col_width = feature_local.shape[1]
    hidden_width = hidden_grad.shape[1]
    relations = adj_local.shape[1]
    initial = jnp.zeros((relations + 1, col_width, hidden_width), jnp.float32)
    piece = lax.all_gather(hidden_grad[None], "feat", axis=0, tiled=True)
    piece_rows = piece.shape[0]
    group_size = math.gcd(piece_rows, 8)
    turn_count = piece_rows // group_size
    word_block = adj_local
    word_block = word_block.reshape((turn_count, group_size) + adj_local.shape[1:])
    column_block = feature_local
    column_block = column_block.reshape((turn_count, group_size) + feature_local.shape[1:])
    grad_block = piece.reshape((turn_count, group_size) + piece.shape[1:])

    def one_turn(running, inputs):
        return (running + panel_terms(inputs[0], inputs[1], inputs[2]), None)

    running, unused = lax.scan(one_turn, initial, (word_block, column_block, grad_block))
    grad_w1 = lax.psum(running, "rep")
    grad_w2, grad_b1, grad_b2 = lax.psum((weight_grad, bias_one, bias_two), ("feat", "rep"))
    return (grad_w1, grad_b1, grad_w2, grad_b2)


def solution(mesh):
    placed = (
        P("rep", None, "feat", None),
        P("rep", None, None, None, None),
        P("rep", "feat", None, None),
        P("rep", "feat", None, None, None),
        P(),
        P("rep", "feat", None, None),
    )
    return jax.shard_map(
        on_device,
        mesh=mesh,
        in_specs=placed,
        out_specs=(P(None, "feat", None), P(), P(), P()),
        check_vma=False,
    )
```

profile of v0, /device:TPU:0, one launch (start us, length us, event | category | flops | bytes accessed | tf_op | source)
XLA Modules:
  0.0 213.1 jit_solution(5158156742498113044)
XLA Ops:
  8.0 0.0 copy-start
  8.0 0.0 all-gather.3.cloned.1.call-start
  8.1 1.6 fusion.28
  9.7 0.1 div.22
  9.8 0.1 shift_right_arithmetic.72
  9.9 0.9 fusion.27
  10.8 1.1 fusion.37
  11.9 2.4 %convert_reduce_fusion = (f32[256]{0:T(256)S(1)}, bf16[256,256]{1,0:T(8,128)(2,1)}) fusion(f32[128,256]{1,0:T(8,128)S(1)} %fusion.37, bf16[5,128,256]{2,1,0:T(8,128)(2,1)S(1)} %fusion.27, bf16[6,256,256]{2,1,0:T(8,128)(2,1)} %param.10, f32[5,128]{1,0:T(8,128)S(1)} %div.22, bf16[1,1,128,256]{3,2,1,0:T(8,128)(2,1)} %param.11, bf16[1,1,256,256]{3,2,1,0:T(8,128)(2,1)} %param.8), kind=kOutput, calls=%fused_computation.38 | convolution fusion | flops 168722176 | bytes 1445376 | tf_op jit(solution)/shard_map/rsd,rsh->dh/dot_general | solution.py:35
  14.4 0.0 all-gather.3.cloned.1.call-update
  14.4 0.0 all-reduce.7.cloned.1.call-start
  14.4 0.9 broadcast_maximum_fusion
  15.4 1.0 convolution_bitcast_fusion.1
  16.4 1.6 fusion.19
  18.0 1.2 pad_maximum_fusion
  19.3 0.0 all-reduce.7.cloned.1.call-update
  19.3 0.2 all-reduce.5.cloned.1.call-start
  19.5 10.9 %and_reduce_fusion = s32[8,5,16,16]{3,2,1,0:T(8,128)S(1)} fusion(s32[8,5,16,512]{3,2,1,0:T(8,128)S(1)} %bitcast.90), kind=kLoop, calls=%fused_computation.3 | loop fusion | flops 15718400 | bytes 1351680 | tf_op jit(solution)/shard_map/while/body/eval_jaxpr/reduce_sum | solution.py:12
  30.4 0.1 maximum_divide_fusion
  30.5 0.2 reshape.90
  30.7 0.1 shift_right_arithmetic.81
  30.7 10.1 %all-gather.3.cloned.1.call-done = bf16[2048,256]{1,0:T(8,128)(2,1)} async-done(((bf16[256,256]{1,0:T(8,128)(2,1)}), bf16[2048,256]{1,0:T(8,128)(2,1)}) %all-gather.3.cloned.1.call-update) | async-done | bytes 1048592 | tf_op jit(solution)/shard_map/all_gather | solution.py:77
  40.9 10.5 %shift_right_arithmetic.78 = s32[8,5,16,16,512]{4,3,2,1,0:T(8,128)} broadcast(s32[8,5,16,512]{3,2,1,0:T(8,128)S(1)} %bitcast.91), dimensions={0,1,2,4} | broadcast | bytes 22282240 | tf_op jit(solution)/shard_map/while/body/eval_jaxpr/shift_right_arithmetic | solution.py:10
  51.3 9.5 %fusion.13 = f32[5,128,256]{2,1,0:T(8,128)S(1)} fusion(bf16[8,256,256,1]{2,1,0,3:T(8,128)(2,1)S(1)} %bitcast.96, f32[8,5,256]{2,0,1:T(8,128)S(1)} %copy.37, s32[8,5,256,512]{3,2,1,0:T(8,128)} %bitcast.89, s32[256]{0:T(256)S(1)} %shift_right_arithmetic.81, bf16[1,8,128,512]{3,2,1,0:T(8,128)(2,1)S(1)} %copy-done.2), kind=kOutput, calls=%fused_computation.14 | convolution fusion | flops 2031616000 | bytes 23766016 | tf_op jit(solution)/shard_map/while/body/eval_jaxpr/brdc,bdh->rch/dot_general | solution.py:56
  60.8 0.5 convolution_bitcast_fusion.2
  61.3 0.1 copy.30
  61.4 1.0 pad_maximum_fusion.1
  62.4 0.0 all-reduce.5.cloned.1.call-update
  62.4 39.3 %all-reduce.1 = (f32[256]{0:T(256)}, f32[256]{0:T(256)}) all-reduce(f32[256]{0:T(256)S(1)} %get-tuple-element.23, f32[256]{0:T(256)S(1)} %fusion.40), channel_id=1, replica_groups=mesh['feat'=8,'rep'=4] {'feat','rep'}, use_global_device_ids=true, to_apply=%region_4.5 | all-reduce | flops 512 | bytes 4096 | tf_op jit(solution)/shard_map/psum | solution.py:92
  101.8 53.7 %all-reduce.7.cloned.1.call-done = f32[6,256,256]{2,1,0:T(8,128)} async-done(((f32[6,256,256]{2,1,0:T(8,128)}), f32[6,256,256]{2,1,0:T(8,128)}) %all-reduce.7.cloned.1.call-update) | async-done | bytes 1572880 | tf_op jit(solution)/shard_map/psum | solution.py:92
  155.4 45.4 %all-reduce.5.cloned.1.call-done = f32[6,128,256]{2,1,0:T(8,128)} async-done(((f32[6,128,256]{2,1,0:T(8,128)}), f32[6,128,256]{2,1,0:T(8,128)}) %all-reduce.5.cloned.1.call-update) | async-done | bytes 786448 | tf_op jit(solution)/shard_map/psum | solution.py:91
  200.8 2.1 copy.52
  202.9 2.7 %copy.53 = f32[6,256,256]{2,1,0:T(8,128)} copy(f32[6,256,256]{2,1,0:T(8,128)} %all-reduce.7.cloned.1.call-done) | data formatting | bytes 3145728
  (12 shorter events, 0.1 us)
Async XLA Ops:
  8.0 11.5 %copy-start = (s32[1,8,5,16,512]{4,3,2,1,0:T(8,128)S(1)}, s32[1,8,5,16,512]{4,3,2,1,0:T(8,128)}, u32[]{:S(2)}) copy-start(s32[1,8,5,16,512]{4,3,2,1,0:T(8,128)} %param.7) | copy-start | bytes 3932164
  8.0 32.9 %all-gather.3.cloned.1.call-start = ((), (), s32[]{:S(2)}) async-start(), calls=%async_computation.2 | async-start | bytes 1179648 | tf_op jit(solution)/shard_map/all_gather | solution.py:77
  14.4 141.0 %all-reduce.7.cloned.1.call-start = ((), (), s32[]{:S(2)}) async-start(), calls=%async_computation.1 | async-start | bytes 3145728 | tf_op jit(solution)/shard_map/psum | solution.py:92
  19.3 181.5 %all-reduce.5.cloned.1.call-start = ((), (), s32[]{:S(2)}) async-start(), calls=%async_computation | async-start | bytes 1572864 | tf_op jit(solution)/shard_map/psum | solution.py:91
  40.9 10.5 %copy-start.2 = (bf16[1,8,128,512]{3,2,1,0:T(8,128)(2,1)S(1)}, bf16[1,8,128,512]{3,2,1,0:T(8,128)(2,1)}, u32[]{:S(2)}) copy-start(bf16[1,8,128,512]{3,2,1,0:T(8,128)(2,1)} %param.6) | copy-start | bytes 3145732
  40.9 10.5 %copy-start.3 = (bf16[2048,256]{1,0:T(8,128)(2,1)S(1)}, bf16[2048,256]{1,0:T(8,128)(2,1)}, u32[]{:S(2)}) copy-start(bf16[2048,256]{1,0:T(8,128)(2,1)} %all-gather.3.cloned.1.call-done) | copy-start | bytes 3145732
  51.3 11.0 %copy-start.1 = (bf16[1,1,128,256]{3,2,1,0:T(8,128)(2,1)S(1)}, bf16[1,1,128,256]{3,2,1,0:T(8,128)(2,1)}, u32[]{:S(2)}) copy-start(bf16[1,1,128,256]{3,2,1,0:T(8,128)(2,1)} %param.11) | copy-start | bytes 196612
Sparse Core Ops, SparseCore 0:
  14.5 26.3 all-gather.2
Sparse Core Ops, SparseCore 1:
  20.7 134.6 all-reduce.6
  158.2 42.5 all-reduce.4
where the time goes:
time: 214 us; the launch traced here: 213 us
  waiting for transfers between devices  109 us (51%)
  blocking collectives  39.3 us (18%)
  other arithmetic  16.6 us (8%)
  matrix products  16.1 us (8%)
  local copies, waits for them, and re-layouts  15.8 us (7%)
  between operations  15.6 us (7%)
    psum x1, waiting for transfers between devices, on_device(): lax.psum((weight_grad, bias_one, bias_two), ('feat', 'rep'))  53.7 us
    psum x1, waiting for transfers between devices, on_device(): grad_w1 = lax.psum(running, 'rep')  45.4 us
    psum x1, blocking collectives, on_device(): lax.psum((weight_grad, bias_one, bias_two), ('feat', 'rep'))  39.3 us
    reduce_sum x1, other arithmetic, unpack(): degree = jnp.sum(dense, axis=-1).astype(jnp.float32)  10.9 us
    shift_right_arithmetic x5, local copies, waits for them, and re-layouts, unpack(): jnp.right_shift(packed[..., None, :], shifts[:, None])  10.6 us
    all_gather x1, waiting for transfers between devices, on_device(): piece = lax.all_gather(hidden_grad[None], 'feat', axis=0, tiled=True)  10.1 us
    dot_general x1, matrix products, panel_terms(): jnp.einsum('brdc,bdh->rch', gathered, grad_block, preferred_element_type=...  9.46 us
    unnamed x10, local copies, waits for them, and re-layouts  4.85 us
  transfers between devices with their start and end apart: 3, of which 3 were waited for; matrix products, arithmetic and copies ran while one was open for 18% of the time, Pallas kernels for 0%

commit v1 on v0

--- a/solution.py
+++ b/solution.py
@@ -89,7 +89,7 @@
 
     running, unused = lax.scan(one_turn, initial, (word_block, column_block, grad_block))
     grad_w1 = lax.psum(running, "rep")
-    grad_w2, grad_b1, grad_b2 = lax.psum((weight_grad, bias_one, bias_two), ("feat", "rep"))
+    grad_w2, grad_b1, grad_b2 = lax.psum(lax.psum((weight_grad, bias_one, bias_two), "rep"), "feat")
     return (grad_w1, grad_b1, grad_w2, grad_b2)
 
 

time: 214 us -> 229 us (1.070)
  waiting for transfers between devices: 109 us -> 145 us
  blocking collectives: 39.3 us -> 22.5 us
    psum x1, waiting for transfers between devices: 45.4 us -> 94.7 us  [on_device(): grad_w1 = lax.psum(running, 'rep')]
    psum x1 -> x2, blocking collectives: 39.3 us -> 22.5 us  [the longest x1 12.5 us: on_device(): lax.psum(lax.psum((weight_grad, bias_one, bias_two), 'rep'), 'feat')]
    psum x1, waiting for transfers between devices: 53.7 us -> 38.6 us  [on_device(): lax.psum(lax.psum((weight_grad, bias_one, bias_two), 'rep'), 'feat')]
  transfers between devices with their start and end apart: 3 -> 3, of which waited for: 3 -> 3; matrix products, arithmetic and copies ran while one was open for 18% -> 7% of each run, Pallas kernels for 0% -> 0%
where the time goes in v1:
time: 229 us
  waiting for transfers between devices  145 us (63%)
  blocking collectives  22.5 us (10%)
  other arithmetic  17.2 us (8%)
  matrix products  15.8 us (7%)
  local copies, waits for them, and re-layouts  15 us (7%)
  between operations  13.9 us (6%)
    psum x1, waiting for transfers between devices, on_device(): grad_w1 = lax.psum(running, 'rep')  94.7 us
    psum x1, waiting for transfers between devices, on_device(): lax.psum(lax.psum((weight_grad, bias_one, bias_two), 'rep'), 'feat')  38.6 us
    psum x1, blocking collectives, on_device(): lax.psum(lax.psum((weight_grad, bias_one, bias_two), 'rep'), 'feat')  12.5 us
    reduce_sum x1, other arithmetic, unpack(): degree = jnp.sum(dense, axis=-1).astype(jnp.float32)  12.3 us
    all_gather x1, waiting for transfers between devices, on_device(): piece = lax.all_gather(hidden_grad[None], 'feat', axis=0, tiled=True)  11.1 us
    psum x1, blocking collectives, on_device(): lax.psum((weight_grad, bias_one, bias_two), 'rep')  9.98 us
    shift_right_arithmetic x5, local copies, waits for them, and re-layouts, unpack(): jnp.right_shift(packed[..., None, :], shifts[:, None])  9.83 us
    dot_general x1, matrix products, panel_terms(): jnp.einsum('brdc,bdh->rch', gathered, grad_block, preferred_element_type=...  9.39 us
  transfers between devices with their start and end apart: 3, of which 3 were waited for; matrix products, arithmetic and copies ran while one was open for 7% of the time, Pallas kernels for 0%

profile of v1, /device:TPU:0, one launch (start us, length us, event | category | flops | bytes accessed | tf_op | source)
XLA Modules:
  0.0 229.1 jit_solution(9579017979459728806)
XLA Ops:
  7.2 0.0 copy-start.1
  7.2 0.0 all-gather.3.cloned.1.call-start
  7.2 1.6 fusion.28
  8.8 0.1 div.22
  8.9 0.1 shift_right_arithmetic.72
  9.0 0.9 fusion.27
  9.9 1.1 fusion.37
  11.1 2.4 %convert_reduce_fusion = (f32[256]{0:T(256)S(1)}, bf16[256,256]{1,0:T(8,128)(2,1)}) fusion(f32[128,256]{1,0:T(8,128)S(1)} %fusion.37, bf16[5,128,256]{2,1,0:T(8,128)(2,1)S(1)} %fusion.27, bf16[6,256,256]{2,1,0:T(8,128)(2,1)} %param.10, f32[5,128]{1,0:T(8,128)S(1)} %div.22, bf16[1,1,128,256]{3,2,1,0:T(8,128)(2,1)} %param.11, bf16[1,1,256,256]{3,2,1,0:T(8,128)(2,1)} %param.8), kind=kOutput, calls=%fused_computation.38 | convolution fusion | flops 168722176 | bytes 1445376 | tf_op jit(solution)/shard_map/rsd,rsh->dh/dot_general | solution.py:35
  13.5 0.0 all-gather.3.cloned.1.call-update
  13.5 0.0 all-reduce.9.cloned.1.call-start
  13.6 12.3 %and_reduce_fusion = s32[8,5,16,16]{3,2,1,0:T(8,128)S(1)} fusion(s32[8,5,16,512]{3,2,1,0:T(8,128)} %bitcast.90), kind=kLoop, calls=%fused_computation.3 | loop fusion | flops 15718400 | bytes 1351680 | tf_op jit(solution)/shard_map/while/body/eval_jaxpr/reduce_sum | solution.py:12
  25.9 0.1 maximum_divide_fusion
  25.9 0.2 reshape.90
  26.1 0.1 shift_right_arithmetic.81
  26.2 0.2 convolution_bitcast_fusion.1
  26.4 0.9 fusion.19
  27.3 1.3 pad_maximum_fusion
  28.6 11.1 %all-gather.3.cloned.1.call-done = bf16[2048,256]{1,0:T(8,128)(2,1)} async-done(((bf16[256,256]{1,0:T(8,128)(2,1)}), bf16[2048,256]{1,0:T(8,128)(2,1)}) %all-gather.3.cloned.1.call-update) | async-done | bytes 1048592 | tf_op jit(solution)/shard_map/all_gather | solution.py:77
  39.8 1.8 convolution_bitcast_fusion.2
  41.6 0.1 copy.30
  41.7 9.7 %shift_right_arithmetic.78 = s32[8,5,16,16,512]{4,3,2,1,0:T(8,128)} broadcast(s32[8,5,16,512]{3,2,1,0:T(8,128)S(1)} %bitcast.91), dimensions={0,1,2,4} | broadcast | bytes 22282240 | tf_op jit(solution)/shard_map/while/body/eval_jaxpr/shift_right_arithmetic | solution.py:10
  51.4 9.4 %fusion.13 = f32[5,128,256]{2,1,0:T(8,128)S(1)} fusion(bf16[8,256,256,1]{2,1,0,3:T(8,128)(2,1)} %bitcast.97, f32[8,5,256]{2,0,1:T(8,128)S(1)} %copy.37, s32[8,5,256,512]{3,2,1,0:T(8,128)} %bitcast.89, s32[256]{0:T(256)S(1)} %shift_right_arithmetic.81, bf16[1,8,128,512]{3,2,1,0:T(8,128)(2,1)S(1)} %copy-done.3), kind=kOutput, calls=%fused_computation.14 | convolution fusion | flops 2031616000 | bytes 23766016 | tf_op jit(solution)/shard_map/while/body/eval_jaxpr/brdc,bdh->rch/dot_general | solution.py:56
  60.8 0.9 pad_maximum_fusion.1
  61.7 0.0 all-reduce.9.cloned.1.call-update
  61.7 0.0 all-reduce.7.cloned.1.call-start
  61.8 94.7 %all-reduce.9.cloned.1.call-done = (f32[6,128,256]{2,1,0:T(8,128)}, f32[6,256,256]{2,1,0:T(8,128)}) async-done(((f32[6,128,256]{2,1,0:T(8,128)}, f32[6,256,256]{2,1,0:T(8,128)}), (f32[6,128,256]{2,1,0:T(8,128)}, f32[6,256,256]{2,1,0:T(8,128)})) %all-reduce.9.cloned.1.call-update) | async-done | bytes 2359312 | tf_op jit(solution)/shard_map/psum | solution.py:91
  156.5 0.0 all-reduce.7.cloned.1.call-update
  156.6 10.0 %all-reduce.2 = (f32[256]{0:T(256)S(1)}, f32[256]{0:T(256)S(1)}) all-reduce(f32[256]{0:T(256)S(1)} %get-tuple-element.27, f32[256]{0:T(256)S(1)} %fusion.40), channel_id=1, replica_groups=mesh['feat'=8,'rep'=4] {'rep'}, use_global_device_ids=true, to_apply=%region_4.5 | all-reduce | flops 512 | bytes 4096 | tf_op jit(solution)/shard_map/psum | solution.py:92
  166.6 12.5 %all-reduce.1 = (f32[256]{0:T(256)}, f32[256]{0:T(256)}) all-reduce(f32[256]{0:T(256)S(1)} %get-tuple-element.21, f32[256]{0:T(256)S(1)} %get-tuple-element.22), channel_id=1, replica_groups=mesh['feat'=8,'rep'=4] {'feat'}, use_global_device_ids=true, to_apply=%region_5.6 | all-reduce | flops 512 | bytes 4096 | tf_op jit(solution)/shard_map/psum | solution.py:92
  179.1 38.6 %all-reduce.7.cloned.1.call-done = f32[6,256,256]{2,1,0:T(8,128)} async-done(((f32[6,256,256]{2,1,0:T(8,128)}), f32[6,256,256]{2,1,0:T(8,128)}) %all-reduce.7.cloned.1.call-update) | async-done | bytes 1572880 | tf_op jit(solution)/shard_map/psum | solution.py:92
  217.7 2.1 copy.53
  219.8 2.7 %copy.54 = f32[6,256,256]{2,1,0:T(8,128)} copy(f32[6,256,256]{2,1,0:T(8,128)} %all-reduce.7.cloned.1.call-done) | data formatting | bytes 3145728
  (13 shorter events, 0.1 us)
Async XLA Ops:
  7.2 19.1 %copy-start.1 = (bf16[1,1,128,256]{3,2,1,0:T(8,128)(2,1)S(1)}, bf16[1,1,128,256]{3,2,1,0:T(8,128)(2,1)}, u32[]{:S(2)}) copy-start(bf16[1,1,128,256]{3,2,1,0:T(8,128)(2,1)} %param.11) | copy-start | bytes 196612
  7.2 19.0 %copy-start.2 = (bf16[1,1,256,256]{3,2,1,0:T(8,128)(2,1)S(1)}, bf16[1,1,256,256]{3,2,1,0:T(8,128)(2,1)}, u32[]{:S(2)}) copy-start(bf16[1,1,256,256]{3,2,1,0:T(8,128)(2,1)} %param.8) | copy-start | bytes 393220
  7.2 32.6 %all-gather.3.cloned.1.call-start = ((), (), s32[]{:S(2)}) async-start(), calls=%async_computation.1 | async-start | bytes 1179648 | tf_op jit(solution)/shard_map/all_gather | solution.py:77
  13.5 28.2 %copy-start = (s32[1,8,5,16,512]{4,3,2,1,0:T(8,128)S(1)}, s32[1,8,5,16,512]{4,3,2,1,0:T(8,128)}, u32[]{:S(2)}) copy-start(s32[1,8,5,16,512]{4,3,2,1,0:T(8,128)} %param.7) | copy-start | bytes 3932164
  13.5 143.0 %all-reduce.9.cloned.1.call-start = ((), (), s32[]{:S(2)}) async-start(), calls=%async_computation.2 | async-start | bytes 4718592 | tf_op jit(solution)/shard_map/psum | solution.py:91
  41.7 9.7 %copy-start.3 = (bf16[1,8,128,512]{3,2,1,0:T(8,128)(2,1)S(1)}, bf16[1,8,128,512]{3,2,1,0:T(8,128)(2,1)}, u32[]{:S(2)}) copy-start(bf16[1,8,128,512]{3,2,1,0:T(8,128)(2,1)} %param.6) | copy-start | bytes 3145732
  61.7 156.0 %all-reduce.7.cloned.1.call-start = ((), (), s32[]{:S(2)}) async-start(), calls=%async_computation | async-start | bytes 3145728 | tf_op jit(solution)/shard_map/psum | solution.py:92
Sparse Core Ops, SparseCore 0:
  13.6 26.0 all-gather.2
  61.9 94.6 all-reduce.8
  159.8 57.8 all-reduce.6
